TPU v7x, 32 devices: a whole 2x2x4 slice. The times are simulated.
32 devices in a mesh: px: 4 (over y, x), py: 8 (over z, core).
Axes of the slice: x: 2, y: 2, z: 4, core: 2. Of those that a mesh axis runs over, the one named last changes fastest.
Arguments:
- coefficients: bfloat16 [384, 12288], P(('px', 'py')), may hold values from -6 to 6
- exponents: int32 [96, 768], P(('px', 'py')), may hold values from -4 to 1
- right_side: float32 [64, 192, 384], P('px', 'py'), may hold values from -18 to 18
Outputs:
- decoded: float32 [64, 192, 384], P('px', 'py')
- residual: float32 [64, 192, 384], P('px', 'py')
- rms: float32 [], replicated
All inputs are finite; a program needn't handle non-finite values.
Results may differ from a plain program's by a relative error of at most 0.0003.
Values may be sent and summed in bfloat16 or wider, within the bound.
No kernel may reach another device: no remote copies, remote signals or barrier semaphores. Data moves between devices by JAX's collectives and lax.ppermute only.
A program may use at most 64 MiB of HBM per device.

v0:
```python
import jax
import jax.numpy as jnp
from jax import lax
from jax.sharding import PartitionSpec as P

CX = 16
CY = 24


def with_halo(cells, sides, width):
    for axis, dim in sides:
        count = lax.axis_size(axis)
        ends = count - 1
        head = lax.slice_in_dim(cells, 0, width, axis=dim)
        tail = lax.slice_in_dim(cells, cells.shape[dim] - width, cells.shape[dim], axis=dim)
        cells = jnp.concatenate(
            [
                lax.ppermute(tail, axis, [(i, (i + 1) % count) for i in range(ends)]),
                cells,
                lax.ppermute(head, axis, [((i + 1) % count, i) for i in range(ends)]),
            ],
            axis=dim,
        )
    return cells


def block_basis(width):
    rows = jnp.arange(width, dtype=jnp.int32)[:, None]
    cols = jnp.arange(width, dtype=jnp.int32)[None, :]
    frequency = (rows % 4).astype(jnp.float32)
    point = (cols % 4).astype(jnp.float32)
    weight = jnp.where(frequency == 0, jnp.sqrt(jnp.float32(0.25)), jnp.sqrt(jnp.float32(0.5)))
    entry = weight * jnp.cos(jnp.pi * (2.0 * point + 1.0) * frequency / 8.0)
    return jnp.where(rows // 4 == cols // 4, entry, 0.0)


def plane_table():
    across_x = block_basis(CX)
    across_y = block_basis(CY)
    return jnp.einsum("ux,vy->uvxy", across_x, across_y).reshape(CX * CY, CX * CY)


def spread_table():
    quarter_y = CY // 4
    blocks = jnp.arange(CX // 4 * quarter_y, dtype=jnp.int32)[:, None]
    cells = jnp.arange(CX * CY, dtype=jnp.int32)[None, :]
    same_x = cells // CY // 4 == blocks // quarter_y
    same_y = cells % CY // 4 == blocks % quarter_y
    return jnp.where(same_x & same_y, 1.0, 0.0).astype(jnp.float32)


def apply_plane(layers, table):
    return jnp.einsum(
        "zpc,cv->zpv", layers.astype(jnp.float32), table, precision=lax.Precision.HIGHEST
    )


def shards(coefficients, exponents, right_side):
    count_x = lax.axis_size("px")
    count_y = lax.axis_size("py")
    peers = count_x * count_y
    patch = CX * CY
    layer_count = coefficients.shape[0]
    block_layers = exponents.shape[0]
    table = plane_table()
    factor = jnp.exp2(exponents.astype(jnp.float32)).reshape(block_layers, peers, -1)
    spread = jnp.einsum("zpq,qc->zpc", factor, spread_table(), precision=lax.Precision.HIGHEST)
    spread = jnp.broadcast_to(spread[:, None], (block_layers, 4, peers, patch)).reshape(
        layer_count, peers, patch
    )
    scaled = (coefficients.astype(jnp.float32).reshape(layer_count, peers, patch) * spread).astype(
        jnp.bfloat16
    )
    received = lax.all_to_all(scaled, ("px", "py"), split_axis=1, concat_axis=1, tiled=True)
    arrived = apply_plane(received, table)
    stacked = arrived.transpose(1, 0, 2).reshape(-1, 128, patch)
    depth_table = block_basis(128)
    decoded = jnp.einsum(
        "nzq,zw->qnw", stacked, depth_table, precision=lax.Precision.HIGHEST
    ).reshape(CX, CY, -1)
    padded = with_halo(decoded, (("px", 0), ("py", 1)), 1)
    padded = jnp.pad(padded, ((0, 0), (0, 0), (1, 1)))
    beside = padded[2:, 1:-1, 1:-1] + padded[:-2, 1:-1, 1:-1]
    beside = beside + padded[1:-1, 2:, 1:-1] + padded[1:-1, :-2, 1:-1]
    beside = beside + padded[1:-1, 1:-1, 2:] + padded[1:-1, 1:-1, :-2]
    residual = right_side - (6.0 * decoded - beside)
    local_sum = jnp.sum(residual * residual)
    total_sum = lax.psum(local_sum, ("px", "py"))
    cell_count = decoded.shape[0] * decoded.shape[1] * decoded.shape[2] * count_x * count_y
    rms = jnp.sqrt(total_sum / cell_count + 1e-06)
    return (decoded, residual, rms)


def solution(mesh):
    return jax.shard_map(
        shards,
        mesh=mesh,
        in_specs=(P(("px", "py"), None), P(("px", "py"), None), P("px", "py", None)),
        out_specs=(P("px", "py", None), P("px", "py", None), P()),
        check_vma=False,
    )
```

profile of v0, /device:TPU:0, one launch (start us, length us, event | category | flops | bytes accessed | tf_op | source)
XLA Modules:
  0.0 87.5 jit_solution(5199137240304117079)
XLA Ops:
  0.7 0.7 multiply_exponential_fusion
  1.4 0.1 reshape.520
  1.5 1.1 %reshape.525 = f32[12,12288]{1,0:T(8,128)S(1)} convert(bf16[12,12288]{1,0:T(8,128)(2,1)} %param.3) | non-fusion elementwise | flops 147456 | bytes 884736 | tf_op jit(solution)/shard_map/reshape | solution.py:71
  2.5 0.2 copy.34
  2.7 0.3 fusion.15
  3.0 0.1 fusion.1
  3.1 0.8 copy.27
  3.9 7.3 %all-to-all-start = ((bf16[12,32,384]{2,0,1:T(8,128)(2,1)}), bf16[12,32,384]{2,0,1:T(8,128)(2,1)S(1)}, u32[]{:S(2)}, u32[]{:S(2)}) async-start(bf16[12,32,384]{2,0,1:T(8,128)(2,1)} %copy.27), calls=%async_computation | async-start | bytes 786432 | tf_op jit(solution)/shard_map/all_to_all | solution.py:74
  11.3 0.1 multiply_select_fusion
  11.5 0.1 multiply_select_fusion.1
  11.6 0.3 multiply_bitcast_fusion
  11.9 2.3 %reshape.528 = f32[384,384,1]{1,0,2:T(8,128)} reshape(f32[16,24,16,24]{3,2,1,0:T(8,128)S(1)} %multiply_bitcast_fusion) | data formatting | bytes 1179648 | tf_op jit(solution)/shard_map/reshape | solution.py:40
  14.3 10.4 %all-to-all-done = bf16[12,32,384]{2,0,1:T(8,128)(2,1)S(1)} async-done(((bf16[12,32,384]{2,0,1:T(8,128)(2,1)}), bf16[12,32,384]{2,0,1:T(8,128)(2,1)S(1)}, u32[]{:S(2)}, u32[]{:S(2)}) %all-to-all-start) | async-done | bytes 294944 | tf_op jit(solution)/shard_map/all_to_all | solution.py:74
  24.7 1.8 %convolution_bitcast_fusion.1 = f32[32,12,384]{2,0,1:T(8,128)S(1)} fusion(f32[384,384,1]{1,0,2:T(8,128)} %reshape.528, bf16[12,32,384]{2,0,1:T(8,128)(2,1)S(1)} %all-to-all-done), kind=kOutput, calls=%fused_computation.4 | convolution fusion | flops 679477248 | bytes 1474560 | tf_op jit(solution)/shard_map/zpc,cv->zpv/dot_general | solution.py:53
  26.5 0.4 copy.29
  26.9 0.1 reshape.523
  27.0 0.9 %convolution_bitcast_fusion = f32[384,3,128]{0,2,1:T(8,128)S(1)} fusion(f32[3,128,384]{2,1,0:T(8,128)S(1)} %reshape.523, f32[128]{0:T(128)S(1)} %get-tuple-element.27, f32[128]{0:T(128)S(1)} %get-tuple-element.25, f32[128]{0:T(128)S(1)} %get-tuple-element.24, s32[128]{0:T(128)S(1)} %get-tuple-element.26), kind=kOutput, calls=%fused_computation.3 | convolution fusion | flops 226574336 | bytes 1181696 | tf_op jit(solution)/shard_map/nzq,zw->qnw/dot_general | solution.py:78
  27.9 0.1 fusion.54
  28.0 0.1 copy.32
  28.1 1.5 %collective-permute-start.1 = (f32[1,24,384]{2,1,0:T(8,128)S(1)}, f32[1,24,384]{2,1,0:T(8,128)S(1)}, u32[]{:S(2)}, u32[]{:S(2)}) collective-permute-start(f32[1,24,384]{2,1,0:T(8,128)S(1)} %copy.32), channel_id=1, source_target_pairs={{0,8},{8,16},{16,24},{1,9},{9,17},{17,25},{2,10},{10,18},{18,26},{... | collective-permute-start | bytes 110600 | tf_op jit(solution)/shard_map/ppermute | solution.py:18
  29.6 0.3 copy.30
  29.9 0.3 reshape.524
  30.3 0.0 copy-start
  30.3 0.1 copy.31
  30.4 1.3 %collective-permute-start = (f32[1,24,384]{2,1,0:T(8,128)S(1)}, f32[1,24,384]{2,1,0:T(8,128)S(1)}, u32[]{:S(2)}, u32[]{:S(2)}) collective-permute-start(f32[1,24,384]{2,1,0:T(8,128)S(1)} %copy.31), channel_id=1, source_target_pairs={{8,0},{16,8},{24,16},{9,1},{17,9},{25,17},{10,2},{18,10},{26,18},{... | collective-permute-start | bytes 110600 | tf_op jit(solution)/shard_map/ppermute | solution.py:20
  31.8 4.9 %collective-permute-done = f32[1,24,384]{2,1,0:T(8,128)S(1)} collective-permute-done((f32[1,24,384]{2,1,0:T(8,128)S(1)}, f32[1,24,384]{2,1,0:T(8,128)S(1)}, u32[]{:S(2)}, u32[]{:S(2)}) %collective-permute-start) | collective-permute-done | bytes 36896 | tf_op jit(solution)/shard_map/ppermute | solution.py:20
  36.8 1.3 %collective-permute-start.2 = (f32[18,1,384]{2,1,0:T(1,128)S(1)}, f32[18,1,384]{2,1,0:T(1,128)S(1)}, u32[]{:S(2)}, u32[]{:S(2)}) collective-permute-start(f32[18,1,384]{2,1,0:T(1,128)S(1)} %get-tuple-element.9), channel_id=1, source_target_pairs={{1,0},{2,1},{3,2},{4,3},{5,4},{6,5},{7,6},{9,8},{10,9},{11,10},{12... | collective-permute-start | bytes 82952 | tf_op jit(solution)/shard_map/ppermute | solution.py:20
  38.1 3.0 %collective-permute-start.3 = (f32[18,1,384]{2,1,0:T(1,128)S(1)}, f32[18,1,384]{2,1,0:T(1,128)S(1)}, u32[]{:S(2)}, u32[]{:S(2)}) collective-permute-start(f32[18,1,384]{2,1,0:T(1,128)S(1)} %get-tuple-element.8), channel_id=1, source_target_pairs={{0,1},{1,2},{2,3},{3,4},{4,5},{5,6},{6,7},{8,9},{9,10},{10,11},{11... | collective-permute-start | bytes 82952 | tf_op jit(solution)/shard_map/ppermute | solution.py:18
  41.1 0.8 collective-permute-done.3
  41.9 0.6 select_maximum_fusion
  42.5 1.9 %multiply_reduce_fusion = (f32[]{:T(128)}, f32[16,24,384]{2,1,0:T(8,128)}) fusion(f32[16,24,384]{2,1,0:T(8,128)S(1)} %copy-done.1, f32[18,26,386]{2,1,0:T(8,128)S(1)} %select_maximum_fusion, f32[18,24,384]{2,1,0:T(8,128)S(1)} %constant_dynamic-update-slice_fusion, f32[18,1,384]{2,1,0:T(1,128)S(1)} %collective-permute-done.3, ...), kind=kLoop, calls=%fused_computation.21 | loop fusion | flops 2064383 | bytes 3741700 | tf_op jit(solution)/shard_map/reduce_sum | solution.py:87
  44.4 41.2 %psum.7 = f32[]{:T(128)} all-reduce(f32[]{:T(128)} %get-tuple-element.6), channel_id=1, replica_groups=mesh['px'=4,'py'=8] {'px','py'}, use_global_device_ids=true, to_apply=%region_1.2 | all-reduce | flops 1 | bytes 8 | tf_op jit(solution)/shard_map/psum | solution.py:88
  (17 shorter events, 0.2 us)
Async XLA Ops:
  3.9 20.8 %all-to-all-start = ((bf16[12,32,384]{2,0,1:T(8,128)(2,1)}), bf16[12,32,384]{2,0,1:T(8,128)(2,1)S(1)}, u32[]{:S(2)}, u32[]{:S(2)}) async-start(bf16[12,32,384]{2,0,1:T(8,128)(2,1)} %copy.27), calls=%async_computation | async-start | bytes 786432 | tf_op jit(solution)/shard_map/all_to_all | solution.py:74
  28.1 3.6 %collective-permute-start.1 = (f32[1,24,384]{2,1,0:T(8,128)S(1)}, f32[1,24,384]{2,1,0:T(8,128)S(1)}, u32[]{:S(2)}, u32[]{:S(2)}) collective-permute-start(f32[1,24,384]{2,1,0:T(8,128)S(1)} %copy.32), channel_id=1, source_target_pairs={{0,8},{8,16},{16,24},{1,9},{9,17},{17,25},{2,10},{10,18},{18,26},{... | collective-permute-start | bytes 110600 | tf_op jit(solution)/shard_map/ppermute | solution.py:18
  30.3 12.3 %copy-start = (f32[16,24,384]{2,1,0:T(8,128)}, f32[16,24,384]{2,1,0:T(8,128)S(1)}, u32[]{:S(2)}) copy-start(f32[16,24,384]{2,1,0:T(8,128)S(1)} %reshape.524) | copy-start | bytes 1769476
  30.4 6.3 %collective-permute-start = (f32[1,24,384]{2,1,0:T(8,128)S(1)}, f32[1,24,384]{2,1,0:T(8,128)S(1)}, u32[]{:S(2)}, u32[]{:S(2)}) collective-permute-start(f32[1,24,384]{2,1,0:T(8,128)S(1)} %copy.31), channel_id=1, source_target_pairs={{8,0},{16,8},{24,16},{9,1},{17,9},{25,17},{10,2},{18,10},{26,18},{... | collective-permute-start | bytes 110600 | tf_op jit(solution)/shard_map/ppermute | solution.py:20
  31.7 10.8 %copy-start.1 = (f32[16,24,384]{2,1,0:T(8,128)S(1)}, f32[16,24,384]{2,1,0:T(8,128)}, u32[]{:S(2)}) copy-start(f32[16,24,384]{2,1,0:T(8,128)} %param.5) | copy-start | bytes 1769476
  36.8 4.3 %collective-permute-start.2 = (f32[18,1,384]{2,1,0:T(1,128)S(1)}, f32[18,1,384]{2,1,0:T(1,128)S(1)}, u32[]{:S(2)}, u32[]{:S(2)}) collective-permute-start(f32[18,1,384]{2,1,0:T(1,128)S(1)} %get-tuple-element.9), channel_id=1, source_target_pairs={{1,0},{2,1},{3,2},{4,3},{5,4},{6,5},{7,6},{9,8},{10,9},{11,10},{12... | collective-permute-start | bytes 82952 | tf_op jit(solution)/shard_map/ppermute | solution.py:20
  38.1 3.9 %collective-permute-start.3 = (f32[18,1,384]{2,1,0:T(1,128)S(1)}, f32[18,1,384]{2,1,0:T(1,128)S(1)}, u32[]{:S(2)}, u32[]{:S(2)}) collective-permute-start(f32[18,1,384]{2,1,0:T(1,128)S(1)} %get-tuple-element.8), channel_id=1, source_target_pairs={{0,1},{1,2},{2,3},{3,4},{4,5},{5,6},{6,7},{8,9},{9,10},{10,11},{11... | collective-permute-start | bytes 82952 | tf_op jit(solution)/shard_map/ppermute | solution.py:18
where the time goes:
time: 88.1 us; the launch traced here: 87.5 us
  blocking collectives  41.2 us (47%)
  waiting for transfers between devices  16.2 us (18%)
  starting transfers between devices  14.5 us (16%)
  other arithmetic  4.98 us (6%)
  local copies, waits for them, and re-layouts  4.87 us (6%)
  matrix products  3.05 us (3%)
  between operations  2.71 us (3%)
    psum x1, blocking collectives, shards(): total_sum = lax.psum(local_sum, ('px', 'py'))  41.2 us
    all_to_all x1, waiting for transfers between devices, shards(): lax.all_to_all(scaled, ('px', 'py'), split_axis=1, concat_axis=1, tiled=T...  10.4 us
    all_to_all x1, starting transfers between devices, shards(): lax.all_to_all(scaled, ('px', 'py'), split_axis=1, concat_axis=1, tiled=T...  7.33 us
    ppermute x2, waiting for transfers between devices, with_halo(): lax.ppermute(head, axis, [((i + 1) % count, i) for i in range(ends)])  4.95 us
    ppermute x2, starting transfers between devices, with_halo(): lax.ppermute(tail, axis, [(i, (i + 1) % count) for i in range(ends)])  4.57 us
    ppermute x2, starting transfers between devices, with_halo(): lax.ppermute(head, axis, [((i + 1) % count, i) for i in range(ends)])  2.59 us
    reshape x1, local copies, waits for them, and re-layouts, plane_table(): jnp.einsum('ux,vy->uvxy', across_x, across_y).reshape(CX * CY, CX * CY)  2.34 us
    reduce_sum x1, other arithmetic, shards(): local_sum = jnp.sum(residual * residual)  1.91 us
  transfers between devices with their start and end apart: 5, of which 3 were waited for; matrix products, arithmetic and copies ran while one was open for 4% of the time, Pallas kernels for 0%

commit v1 on v0

--- a/solution.py
+++ b/solution.py
@@ -71,7 +71,12 @@
     scaled = (coefficients.astype(jnp.float32).reshape(layer_count, peers, patch) * spread).astype(
         jnp.bfloat16
     )
-    received = lax.all_to_all(scaled, ("px", "py"), split_axis=1, concat_axis=1, tiled=True)
+    received = jnp.concatenate(
+        lax.all_to_all(
+            jnp.stack(jnp.split(scaled, lax.axis_size(("px", "py")), axis=1)), ("px", "py"), 0, 0
+        ),
+        axis=1,
+    )
     arrived = apply_plane(received, table)
     stacked = arrived.transpose(1, 0, 2).reshape(-1, 128, patch)
     depth_table = block_basis(128)

time: 88.1 us -> 106 us (1.20)
  local copies, waits for them, and re-layouts: 4.87 us -> 23.8 us
    unnamed x7 -> x40, local copies, waits for them, and re-layouts: 0.21 us -> 18.9 us
where the time goes in v1:
time: 106 us
  blocking collectives  41.2 us (39%)
  local copies, waits for them, and re-layouts  23.8 us (22%)
  waiting for transfers between devices  16.2 us (15%)
  starting transfers between devices  14.5 us (14%)
  other arithmetic  4.28 us (4%)
  matrix products  3.05 us (3%)
  between operations  2.75 us (3%)
    psum x1, blocking collectives, shards(): total_sum = lax.psum(local_sum, ('px', 'py'))  41.2 us
    unnamed x40, local copies, waits for them, and re-layouts  18.9 us
    all_to_all x1, waiting for transfers between devices, shards(): lax.all_to_all(jnp.stack(jnp.split(scaled, lax.axis_size(('px', 'py')), a...  10.4 us
    all_to_all x1, starting transfers between devices, shards(): lax.all_to_all(jnp.stack(jnp.split(scaled, lax.axis_size(('px', 'py')), a...  7.33 us
    ppermute x2, waiting for transfers between devices, with_halo(): lax.ppermute(head, axis, [((i + 1) % count, i) for i in range(ends)])  4.95 us
    ppermute x2, starting transfers between devices, with_halo(): lax.ppermute(tail, axis, [(i, (i + 1) % count) for i in range(ends)])  4.57 us
    ppermute x2, starting transfers between devices, with_halo(): lax.ppermute(head, axis, [((i + 1) % count, i) for i in range(ends)])  2.59 us
    reshape x1, local copies, waits for them, and re-layouts, plane_table(): jnp.einsum('ux,vy->uvxy', across_x, across_y).reshape(CX * CY, CX * CY)  2.34 us
  transfers between devices with their start and end apart: 5, of which 3 were waited for; matrix products, arithmetic and copies ran while one was open for 4% of the time, Pallas kernels for 0%

profile of v1, /device:TPU:0, one launch (start us, length us, event | category | flops | bytes accessed | tf_op | source)
XLA Modules:
  0.0 105.8 jit_solution(1550527190100074979)
XLA Ops:
  0.7 1.1 reshape.533
  2.9 0.6 constant_dynamic-update-slice_fusion.31
  3.5 0.6 constant_dynamic-update-slice_fusion.30
  4.1 0.6 constant_dynamic-update-slice_fusion.29
  4.7 0.6 constant_dynamic-update-slice_fusion.28
  5.3 0.6 constant_dynamic-update-slice_fusion.27
  8.4 0.6 constant_dynamic-update-slice_fusion.22
  9.0 0.6 constant_dynamic-update-slice_fusion.21
  9.6 0.6 constant_dynamic-update-slice_fusion.20
  10.2 0.6 constant_dynamic-update-slice_fusion.19
  10.8 0.6 constant_dynamic-update-slice_fusion.18
  13.8 0.6 constant_dynamic-update-slice_fusion.13
  14.4 0.6 constant_dynamic-update-slice_fusion.12
  15.0 0.6 constant_dynamic-update-slice_fusion.11
  15.6 0.6 constant_dynamic-update-slice_fusion.10
  16.2 0.6 constant_dynamic-update-slice_fusion.9
  16.8 0.6 constant_dynamic-update-slice_fusion.8
  19.8 0.6 constant_dynamic-update-slice_fusion.3
  20.4 0.6 constant_dynamic-update-slice_fusion.2
  22.2 7.3 %all-to-all-start = ((bf16[32,12,1,384]{3,1,2,0:T(8,128)(2,1)}), bf16[32,12,1,384]{3,1,2,0:T(8,128)(2,1)S(1)}, u32[]{:S(2)}, u32[]{:S(2)}) async-start(bf16[32,12,1,384]{3,1,2,0:T(8,128)(2,1)} %constant_dynamic-update-slice_fusion), calls=%async_computation | async-start | bytes 786432 | tf_op jit(solution)/shard_map/all_to_all | solution.py:75
  30.2 2.3 %reshape.536 = f32[384,384,1]{1,0,2:T(8,128)} reshape(f32[16,24,16,24]{3,2,1,0:T(8,128)S(1)} %multiply_bitcast_fusion) | data formatting | bytes 1179648 | tf_op jit(solution)/shard_map/reshape | solution.py:40
  32.6 10.4 %all-to-all-done = bf16[32,12,1,384]{3,1,2,0:T(8,128)(2,1)S(1)} async-done(((bf16[32,12,1,384]{3,1,2,0:T(8,128)(2,1)}), bf16[32,12,1,384]{3,1,2,0:T(8,128)(2,1)S(1)}, u32[]{:S(2)}, u32[]{:S(2)}) %all-to-all-start) | async-done | bytes 294944 | tf_op jit(solution)/shard_map/all_to_all | solution.py:75
  43.0 1.8 %convolution_bitcast_fusion.1 = f32[32,12,384]{2,0,1:T(8,128)S(1)} fusion(f32[384,384,1]{1,0,2:T(8,128)} %reshape.536, bf16[12,32,1,384]{3,0,2,1:T(8,128)(2,1)S(1)} %bitcast.94), kind=kOutput, calls=%fused_computation.4 | convolution fusion | flops 679477248 | bytes 1474560 | tf_op jit(solution)/shard_map/zpc,cv->zpv/dot_general | solution.py:53
  45.2 0.9 convolution_bitcast_fusion
  46.4 1.5 %collective-permute-start.1 = (f32[1,24,384]{2,1,0:T(8,128)S(1)}, f32[1,24,384]{2,1,0:T(8,128)S(1)}, u32[]{:S(2)}, u32[]{:S(2)}) collective-permute-start(f32[1,24,384]{2,1,0:T(8,128)S(1)} %copy.1191), channel_id=1, source_target_pairs={{0,8},{8,16},{16,24},{1,9},{9,17},{17,25},{2,10},{10,18},{18,26},{... | collective-permute-start | bytes 110600 | tf_op jit(solution)/shard_map/ppermute | solution.py:18
  48.6 1.3 %collective-permute-start = (f32[1,24,384]{2,1,0:T(8,128)S(1)}, f32[1,24,384]{2,1,0:T(8,128)S(1)}, u32[]{:S(2)}, u32[]{:S(2)}) collective-permute-start(f32[1,24,384]{2,1,0:T(8,128)S(1)} %copy.1190), channel_id=1, source_target_pairs={{8,0},{16,8},{24,16},{9,1},{17,9},{25,17},{10,2},{18,10},{26,18},{... | collective-permute-start | bytes 110600 | tf_op jit(solution)/shard_map/ppermute | solution.py:20
  50.0 4.9 %collective-permute-done = f32[1,24,384]{2,1,0:T(8,128)S(1)} collective-permute-done((f32[1,24,384]{2,1,0:T(8,128)S(1)}, f32[1,24,384]{2,1,0:T(8,128)S(1)}, u32[]{:S(2)}, u32[]{:S(2)}) %collective-permute-start) | collective-permute-done | bytes 36896 | tf_op jit(solution)/shard_map/ppermute | solution.py:20
  55.0 1.3 %collective-permute-start.2 = (f32[18,1,384]{2,1,0:T(1,128)S(1)}, f32[18,1,384]{2,1,0:T(1,128)S(1)}, u32[]{:S(2)}, u32[]{:S(2)}) collective-permute-start(f32[18,1,384]{2,1,0:T(1,128)S(1)} %get-tuple-element.9), channel_id=1, source_target_pairs={{1,0},{2,1},{3,2},{4,3},{5,4},{6,5},{7,6},{9,8},{10,9},{11,10},{12... | collective-permute-start | bytes 82952 | tf_op jit(solution)/shard_map/ppermute | solution.py:20
  56.3 3.0 %collective-permute-start.3 = (f32[18,1,384]{2,1,0:T(1,128)S(1)}, f32[18,1,384]{2,1,0:T(1,128)S(1)}, u32[]{:S(2)}, u32[]{:S(2)}) collective-permute-start(f32[18,1,384]{2,1,0:T(1,128)S(1)} %get-tuple-element.8), channel_id=1, source_target_pairs={{0,1},{1,2},{2,3},{3,4},{4,5},{5,6},{6,7},{8,9},{9,10},{10,11},{11... | collective-permute-start | bytes 82952 | tf_op jit(solution)/shard_map/ppermute | solution.py:18
  59.4 0.8 collective-permute-done.3
  60.8 1.9 %multiply_reduce_fusion = (f32[]{:T(128)}, f32[16,24,384]{2,1,0:T(8,128)}) fusion(f32[16,24,384]{2,1,0:T(8,128)S(1)} %copy-done.1, f32[18,26,386]{2,1,0:T(8,128)S(1)} %select_maximum_fusion, f32[18,24,384]{2,1,0:T(8,128)S(1)} %constant_dynamic-update-slice_fusion.32, f32[18,1,384]{2,1,0:T(1,128)S(1)} %collective-permute-done.3, ...), kind=kLoop, calls=%fused_computation.21 | loop fusion | flops 2064383 | bytes 3741700 | tf_op jit(solution)/shard_map/reduce_sum | solution.py:92
  62.7 41.2 %psum.7 = f32[]{:T(128)} all-reduce(f32[]{:T(128)} %get-tuple-element.6), channel_id=1, replica_groups=mesh['px'=4,'py'=8] {'px','py'}, use_global_device_ids=true, to_apply=%region_1.2 | all-reduce | flops 1 | bytes 8 | tf_op jit(solution)/shard_map/psum | solution.py:93
  (52 shorter events, 12.3 us)
Async XLA Ops:
  0.7 1.2 %copy-start.2 = (s32[3,768]{1,0:T(4,128)S(1)}, s32[3,768]{1,0:T(4,128)}, u32[]{:S(2)}) copy-start(s32[3,768]{1,0:T(4,128)} %param.4) | copy-start | bytes 27652
  22.2 20.8 %all-to-all-start = ((bf16[32,12,1,384]{3,1,2,0:T(8,128)(2,1)}), bf16[32,12,1,384]{3,1,2,0:T(8,128)(2,1)S(1)}, u32[]{:S(2)}, u32[]{:S(2)}) async-start(bf16[32,12,1,384]{3,1,2,0:T(8,128)(2,1)} %constant_dynamic-update-slice_fusion), calls=%async_computation | async-start | bytes 786432 | tf_op jit(solution)/shard_map/all_to_all | solution.py:75
  46.4 3.6 %collective-permute-start.1 = (f32[1,24,384]{2,1,0:T(8,128)S(1)}, f32[1,24,384]{2,1,0:T(8,128)S(1)}, u32[]{:S(2)}, u32[]{:S(2)}) collective-permute-start(f32[1,24,384]{2,1,0:T(8,128)S(1)} %copy.1191), channel_id=1, source_target_pairs={{0,8},{8,16},{16,24},{1,9},{9,17},{17,25},{2,10},{10,18},{18,26},{... | collective-permute-start | bytes 110600 | tf_op jit(solution)/shard_map/ppermute | solution.py:18
  48.5 12.3 %copy-start = (f32[16,24,384]{2,1,0:T(8,128)}, f32[16,24,384]{2,1,0:T(8,128)S(1)}, u32[]{:S(2)}) copy-start(f32[16,24,384]{2,1,0:T(8,128)S(1)} %reshape.532) | copy-start | bytes 1769476
  48.6 6.3 %collective-permute-start = (f32[1,24,384]{2,1,0:T(8,128)S(1)}, f32[1,24,384]{2,1,0:T(8,128)S(1)}, u32[]{:S(2)}, u32[]{:S(2)}) collective-permute-start(f32[1,24,384]{2,1,0:T(8,128)S(1)} %copy.1190), channel_id=1, source_target_pairs={{8,0},{16,8},{24,16},{9,1},{17,9},{25,17},{10,2},{18,10},{26,18},{... | collective-permute-start | bytes 110600 | tf_op jit(solution)/shard_map/ppermute | solution.py:20
  50.0 10.8 %copy-start.1 = (f32[16,24,384]{2,1,0:T(8,128)S(1)}, f32[16,24,384]{2,1,0:T(8,128)}, u32[]{:S(2)}) copy-start(f32[16,24,384]{2,1,0:T(8,128)} %param.5) | copy-start | bytes 1769476
  55.0 4.3 %collective-permute-start.2 = (f32[18,1,384]{2,1,0:T(1,128)S(1)}, f32[18,1,384]{2,1,0:T(1,128)S(1)}, u32[]{:S(2)}, u32[]{:S(2)}) collective-permute-start(f32[18,1,384]{2,1,0:T(1,128)S(1)} %get-tuple-element.9), channel_id=1, source_target_pairs={{1,0},{2,1},{3,2},{4,3},{5,4},{6,5},{7,6},{9,8},{10,9},{11,10},{12... | collective-permute-start | bytes 82952 | tf_op jit(solution)/shard_map/ppermute | solution.py:20
  56.3 3.9 %collective-permute-start.3 = (f32[18,1,384]{2,1,0:T(1,128)S(1)}, f32[18,1,384]{2,1,0:T(1,128)S(1)}, u32[]{:S(2)}, u32[]{:S(2)}) collective-permute-start(f32[18,1,384]{2,1,0:T(1,128)S(1)} %get-tuple-element.8), channel_id=1, source_target_pairs={{0,1},{1,2},{2,3},{3,4},{4,5},{5,6},{6,7},{8,9},{9,10},{10,11},{11... | collective-permute-start | bytes 82952 | tf_op jit(solution)/shard_map/ppermute | solution.py:18
